TPU v7x, 32 devices: a whole 2x2x4 slice. The times are simulated.
32 devices in a mesh: shard: 8 (over z, x), rep: 4 (over y, core).
Axes of the slice: x: 2, y: 2, z: 4, core: 2. Of those that a mesh axis runs over, the one named last changes fastest.
Arguments:
- lender_block: int32 [96, 8], P(('shard', 'rep')), may hold values from 0 to 255, as said below
- confidence: bfloat16 [96, 8, 256, 256], P(('shard', 'rep')), may hold values from 0 to 80, as said below
- lender_factors: bfloat16 [65536, 128], P('shard'), may hold values from -4 to 4
Outputs:
- borrower_factors: float32 [24576, 128], P(('shard', 'rep'))
- lender_rhs: float32 [65536, 128], P('shard')
Inputs may be any that keep to these rules, and one draw needn't show every extreme that they name: `lender_block`: within one device's 3 borrower blocks, at most 6 of the 3 x 8 entries name blocks of any one owner (block // 32), and on every device some owner is named exactly 6 times. `confidence`: about half the entries are zero; the others are positive.
All inputs are finite; a program needn't handle non-finite values.
Results may differ from a plain program's by a relative error of at most 0.0047.
Values may be sent and summed in bfloat16 or wider, within the bound.
A program may use at most 128 MiB of HBM per device.

v0:
```python
import jax
import jax.numpy as jnp
from jax import lax
from jax.sharding import PartitionSpec as P

CG_STEPS = 3
HIGH = lax.Precision.HIGHEST


def apply_system(direction, confidence, fetched, gram):
    low = direction.astype(jnp.bfloat16)
    scores = jnp.einsum("btr,bklr->bktl", low, fetched, preferred_element_type=jnp.float32)
    weighted = (confidence.astype(jnp.float32) * scores).astype(jnp.bfloat16)
    back = jnp.einsum("bktl,bklr->btr", weighted, fetched, preferred_element_type=jnp.float32)
    width = direction.shape[-1]
    global_part = jnp.dot(
        direction.reshape(-1, width), gram, precision=HIGH, preferred_element_type=jnp.float32
    )
    return global_part.reshape(direction.shape) + 0.1 * direction + back


def per_device(lender_block, confidence, lender_factors):
    shards = lax.axis_size("shard")
    blocks, lists = lender_block.shape
    tile = confidence.shape[2]
    rank = lender_factors.shape[1]
    owned = lender_factors.shape[0] // tile
    entries = blocks * lists
    slots = (2 * entries + shards - 1) // shards
    local_gram = lax.dot_general(
        lender_factors, lender_factors, (((0,), (0,)), ((), ())), preferred_element_type=jnp.float32
    )
    gram = lax.psum(local_gram, "shard")
    flat = lender_block.reshape(entries)
    owner = flat // owned
    within = flat - owner * owned
    member = (owner[:, None] == jnp.arange(shards, dtype=jnp.int32)[None, :]).astype(jnp.int32)
    position = jnp.sum(jnp.cumsum(member, axis=0) * member, axis=1) - 1
    slot_index = owner * slots + position
    requests = (
        jnp.zeros((shards * slots,), jnp.int32).at[slot_index].set(within).reshape(shards, slots)
    )
    table = lender_factors.reshape(owned, tile, rank)
    incoming = lax.all_to_all(requests, "shard", split_axis=0, concat_axis=0, tiled=True)
    replies = lax.all_to_all(table[incoming], "shard", split_axis=0, concat_axis=0, tiled=True)
    fetched = replies.reshape(shards * slots, tile, rank)[slot_index].reshape(
        blocks, lists, tile, rank
    )
    rhs = jnp.einsum("bktl,bklr->btr", confidence, fetched, preferred_element_type=jnp.float32)
    solution = jnp.zeros_like(rhs)
    resid = rhs
    direction = rhs
    norm_now = jnp.sum(resid * resid, axis=2, keepdims=True)
    for count in range(CG_STEPS):
        image = apply_system(direction, confidence, fetched, gram)
        alpha = norm_now / (jnp.sum(direction * image, axis=2, keepdims=True) + 1e-06)
        solution = solution + alpha * direction
        resid = resid - alpha * image
        norm_next = jnp.sum(resid * resid, axis=2, keepdims=True)
        direction = resid + norm_next / (norm_now + 1e-06) * direction
        norm_now = norm_next
    solved = solution.astype(jnp.bfloat16)
    partial_rhs = jnp.einsum(
        "bktl,btr->bklr", confidence, solved, preferred_element_type=jnp.float32
    )
    outgoing = (
        jnp.zeros((shards * slots, tile, rank), jnp.float32)
        .at[slot_index]
        .set(partial_rhs.reshape(entries, tile, rank))
    )
    returned = lax.all_to_all(
        outgoing.reshape(shards, slots, tile, rank),
        "shard",
        split_axis=0,
        concat_axis=0,
        tiled=True,
    )
    selector = (
        incoming.reshape(-1)[None, :] == jnp.arange(owned, dtype=jnp.int32)[:, None]
    ).astype(jnp.float32)
    owner_sum = jnp.dot(
        selector,
        returned.reshape(shards * slots, tile * rank),
        precision=HIGH,
        preferred_element_type=jnp.float32,
    )
    total = lax.psum(owner_sum, "rep")
    lenders_all = owned * tile * shards
    lender_rhs = total.reshape(owned * tile, rank) / lenders_all
    return (solution.reshape(blocks * tile, rank), lender_rhs)


def solution(mesh):
    in_specs = (P(("shard", "rep"), None), P(("shard", "rep"), None, None, None), P("shard", None))
    out_specs = (P(("shard", "rep"), None), P("shard", None))
    return jax.shard_map(
        per_device, mesh=mesh, in_specs=in_specs, out_specs=out_specs, check_vma=False
    )
```

profile of v0, /device:TPU:0, one launch (start us, length us, event | category | flops | bytes accessed | tf_op | source)
XLA Modules:
  0.0 416.2 jit_solution(9014133852448018927)
XLA Ops:
  7.2 0.0 copy-start
  7.2 0.9 reshape.224
  8.1 0.8 reshape.223
  8.9 0.1 fusion.50
  9.0 0.2 select_reduce_fusion
  9.2 0.6 scatter_custom_fusion
  9.8 0.1 all_to_all.14
  9.9 13.6 %all_to_all.22 = s32[8,1,6]{2,1,0:T(1,128)S(1)} all-to-all(s32[8,1,6]{2,1,0:T(1,128)S(1)} %bitcast.112), channel_id=1, replica_groups=mesh['shard'=8,'rep'=4] {'shard'}, dimensions={0} | all-to-all | bytes 384 | tf_op jit(solution)/shard_map/all_to_all | solution.py:44
  23.5 0.1 copy.32
  23.6 0.1 copy.33
  23.7 0.1 reshape.233
  23.8 2.7 gather_fusion
  26.5 4.4 %all-to-all-start.1 = ((bf16[8,6,256,128]{3,2,1,0:T(8,128)(2,1)}), bf16[8,6,256,128]{3,2,1,0:T(8,128)(2,1)}, u32[]{:S(2)}, u32[]{:S(2)}) async-start(bf16[8,6,256,128]{3,2,1,0:T(8,128)(2,1)} %bitcast.106), calls=%async_computation.1 | async-start | bytes 6291456 | tf_op jit(solution)/shard_map/all_to_all | solution.py:45
  30.9 0.0 all-reduce.3.cloned.1.call-start
  31.0 1.4 fusion.55
  32.4 0.0 all-reduce.3.cloned.1.call-update
  32.4 4.7 %copy.37 = bf16[3,8,256,256]{2,3,1,0:T(8,128)(2,1)} copy(bf16[3,8,256,256]{3,2,1,0:T(8,128)(2,1)} %param.4) | data formatting | bytes 6291456 | tf_op args[1]
  37.1 64.9 %all-to-all-done.1 = bf16[8,6,256,128]{3,2,1,0:T(8,128)(2,1)} async-done(((bf16[8,6,256,128]{3,2,1,0:T(8,128)(2,1)}), bf16[8,6,256,128]{3,2,1,0:T(8,128)(2,1)}, u32[]{:S(2)}, u32[]{:S(2)}) %all-to-all-start.1) | async-done | bytes 3145760 | tf_op jit(solution)/shard_map/all_to_all | solution.py:45
  102.0 3.8 gather_fusion.1
  105.8 3.5 convolution_bitcast_fusion
  109.4 4.3 %fusion.18 = f32[3,256,128]{1,2,0:T(8,128)S(1)} fusion(bf16[3,8,256,128]{3,2,1,0:T(8,128)(2,1)} %bitcast.108, bf16[3,8,256,256]{2,3,1,0:T(8,128)(2,1)} %copy.37, f32[3,256,128]{1,2,0:T(8,128)S(1)} %convolution_bitcast_fusion), kind=kOutput, calls=%fused_computation.20 | convolution fusion | flops 810123264 | bytes 5505024 | tf_op jit(solution)/shard_map/bktl,bklr->btr/dot_general | solution.py:14
  113.7 13.5 %all-reduce.3.cloned.1.call-done = f32[128,128]{1,0:T(8,128)} async-done(((f32[128,128]{1,0:T(8,128)}), f32[128,128]{1,0:T(8,128)}) %all-reduce.3.cloned.1.call-update) | async-done | bytes 65552 | tf_op jit(solution)/shard_map/psum | solution.py:33
  127.2 1.4 multiply_reduce_fusion.3
  128.6 0.1 multiply_reduce_fusion.2
  128.7 0.1 multiply_add_fusion.2
  128.8 5.1 %fusion.21 = f32[3,256,128]{1,2,0:T(8,128)} fusion(bf16[3,8,256,128]{3,2,1,0:T(8,128)(2,1)} %bitcast.109, bf16[3,8,256,256]{2,3,1,0:T(8,128)(2,1)} %copy.37, f32[3,256,128]{1,2,0:T(8,128)S(1)} %multiply_add_fusion.2), kind=kOutput, calls=%fused_computation.21 | convolution fusion | flops 810123264 | bytes 5505024 | tf_op jit(solution)/shard_map/bktl,bklr->btr/dot_general | solution.py:14
  133.8 1.6 multiply_reduce_fusion.1
  135.4 0.1 multiply_reduce_fusion
  135.5 0.8 multiply_add_fusion.1
  136.3 5.2 %fusion.24 = f32[3,256,128]{1,2,0:T(8,128)} fusion(bf16[3,8,256,128]{3,2,1,0:T(8,128)(2,1)} %bitcast.110, bf16[3,8,256,256]{2,3,1,0:T(8,128)(2,1)} %copy.37, f32[3,256,128]{1,2,0:T(8,128)} %multiply_add_fusion.1), kind=kOutput, calls=%fused_computation.22 | convolution fusion | flops 810123264 | bytes 5505024 | tf_op jit(solution)/shard_map/bktl,bklr->btr/dot_general | solution.py:14
  141.5 1.6 fusion.31
  143.1 1.1 multiply_add_fusion
  144.2 4.1 fusion.38
  148.3 3.6 copy.52
  151.9 3.4 broadcast_in_dim.5
  155.3 7.9 %scatter_fusion = f32[48,256,128]{2,1,0:T(8,128)} fusion(f32[48,256,128]{2,1,0:T(8,128)} %broadcast_in_dim.5, s32[24]{0:T(128)S(1)} %fusion.52, f32[24,256,128]{2,1,0:T(8,128)} %copy.52), kind=kCustom, calls=%fused_computation.3 | custom fusion | bytes 9437280 | tf_op jit(solution)/shard_map/scatter | solution.py:69
  163.3 4.8 %all-to-all-start.2 = ((f32[8,6,256,128]{3,2,1,0:T(8,128)}), f32[8,6,256,128]{3,2,1,0:T(8,128)}, u32[]{:S(2)}, u32[]{:S(2)}) async-start(f32[8,6,256,128]{3,2,1,0:T(8,128)} %bitcast.104), calls=%async_computation.2 | async-start | bytes 12582912 | tf_op jit(solution)/shard_map/all_to_all | solution.py:71
  168.0 0.2 all-reduce.5.cloned.1.call-start
  168.2 0.5 broadcast.206
  168.8 0.7 reduce.3
  169.4 0.1 eq.31
  169.5 135.1 %all-to-all-done.2 = f32[8,6,256,128]{3,2,1,0:T(8,128)} async-done(((f32[8,6,256,128]{3,2,1,0:T(8,128)}), f32[8,6,256,128]{3,2,1,0:T(8,128)}, u32[]{:S(2)}, u32[]{:S(2)}) %all-to-all-start.2) | async-done | bytes 6291488 | tf_op jit(solution)/shard_map/all_to_all | solution.py:71
  304.6 10.8 %fusion.3 = f32[32,32768]{1,0:T(8,128)} fusion(f32[6,8,256,128]{3,2,1,0:T(8,128)} %bitcast.40, s32[48]{0:T(128)S(1)} %eq.31), kind=kOutput, calls=%fused_computation.10 | convolution fusion | flops 603981312 | bytes 10485952 | tf_op jit(solution)/shard_map/dot_general | solution.py:81
  315.4 0.0 all-reduce.5.cloned.1.call-update
  315.4 0.9 copy.51
  316.3 83.7 %all-reduce.5.cloned.1.call-done = f32[32,32768]{1,0:T(8,128)} async-done(((f32[32,32768]{1,0:T(8,128)}), f32[32,32768]{1,0:T(8,128)}) %all-reduce.5.cloned.1.call-update) | async-done | bytes 4194320 | tf_op jit(solution)/shard_map/psum | solution.py:87
  400.0 4.4 %broadcast_multiply_fusion = f32[32,32768]{1,0:T(8,128)} fusion(f32[32,32768]{1,0:T(8,128)} %all-reduce.5.cloned.1.call-done), kind=kLoop, calls=%fused_computation.19 | loop fusion | flops 1048576 | bytes 8388608 | tf_op jit(solution)/shard_map/div | solution.py:89
  404.5 4.9 %div.83 = f32[8192,128]{1,0:T(8,128)} reshape(f32[32,32768]{1,0:T(8,128)} %broadcast_multiply_fusion) | data formatting | bytes 8388608 | tf_op jit(solution)/shard_map/div | solution.py:89
  (16 shorter events, 0.1 us)
Async XLA Ops:
  7.2 16.6 %copy-start = (bf16[8192,128]{1,0:T(8,128)(2,1)S(1)}, bf16[8192,128]{1,0:T(8,128)(2,1)}, u32[]{:S(2)}) copy-start(bf16[8192,128]{1,0:T(8,128)(2,1)} %param.5) | copy-start | bytes 6291460
  26.5 75.5 %all-to-all-start.1 = ((bf16[8,6,256,128]{3,2,1,0:T(8,128)(2,1)}), bf16[8,6,256,128]{3,2,1,0:T(8,128)(2,1)}, u32[]{:S(2)}, u32[]{:S(2)}) async-start(bf16[8,6,256,128]{3,2,1,0:T(8,128)(2,1)} %bitcast.106), calls=%async_computation.1 | async-start | bytes 6291456 | tf_op jit(solution)/shard_map/all_to_all | solution.py:45
  30.9 96.2 %all-reduce.3.cloned.1.call-start = ((), (), s32[]{:S(2)}) async-start(), calls=%async_computation.3 | async-start | bytes 131072 | tf_op jit(solution)/shard_map/psum | solution.py:33
  128.7 5.1 %copy-start.2 = (f32[128,128]{1,0:T(8,128)S(1)}, f32[128,128]{1,0:T(8,128)}, u32[]{:S(2)}) copy-start(f32[128,128]{1,0:T(8,128)} %all-reduce.3.cloned.1.call-done) | copy-start | bytes 196612
  136.3 5.2 %copy-start.1 = (f32[3,256,128]{1,2,0:T(8,128)S(1)}, f32[3,256,128]{1,2,0:T(8,128)}, u32[]{:S(2)}) copy-start(f32[3,256,128]{1,2,0:T(8,128)} %multiply_add_fusion.1) | copy-start | bytes 1179652
  163.3 141.3 %all-to-all-start.2 = ((f32[8,6,256,128]{3,2,1,0:T(8,128)}), f32[8,6,256,128]{3,2,1,0:T(8,128)}, u32[]{:S(2)}, u32[]{:S(2)}) async-start(f32[8,6,256,128]{3,2,1,0:T(8,128)} %bitcast.104), calls=%async_computation.2 | async-start | bytes 12582912 | tf_op jit(solution)/shard_map/all_to_all | solution.py:71
  168.0 232.0 %all-reduce.5.cloned.1.call-start = ((), (), s32[]{:S(2)}) async-start(), calls=%async_computation.4 | async-start | bytes 8388608 | tf_op jit(solution)/shard_map/psum | solution.py:87
Sparse Core Ops, SparseCore 0:
  35.7 91.3 all-reduce.2
  315.5 84.4 all-reduce.4
where the time goes:
time: 417 us; the launch traced here: 416 us
  waiting for transfers between devices  297 us (71%)
  matrix products  39 us (9%)
  local copies, waits for them, and re-layouts  35.2 us (8%)
  between operations  14.2 us (3%)
  blocking collectives  13.6 us (3%)
  starting transfers between devices  9.46 us (2%)
  other arithmetic  7.59 us (2%)
    all_to_all x1, waiting for transfers between devices, per_device(): lax.all_to_all(outgoing.reshape(shards, slots, tile, rank), 'shard', spli...  135 us
    psum x1, waiting for transfers between devices, per_device(): total = lax.psum(owner_sum, 'rep')  83.7 us
    all_to_all x1, waiting for transfers between devices, per_device(): lax.all_to_all(table[incoming], 'shard', split_axis=0, concat_axis=0, til...  64.9 us
    dot_general x3, matrix products, apply_system(): jnp.einsum('bktl,bklr->btr', weighted, fetched, preferred_element_type=jn...  14.5 us
    all_to_all x1, blocking collectives, per_device(): lax.all_to_all(requests, 'shard', split_axis=0, concat_axis=0, tiled=True)  13.6 us
    psum x1, waiting for transfers between devices, per_device(): gram = lax.psum(local_gram, 'shard')  13.5 us
    dot_general x1, matrix products, per_device(): jnp.dot(selector, returned.reshape(shards * slots, tile * rank), precisio...  10.8 us
  transfers between devices with their start and end apart: 4, of which 4 were waited for; matrix products, arithmetic and copies ran while one was open for 5% of the time, Pallas kernels for 0%

commit v1 on v0

--- a/solution.py
+++ b/solution.py
@@ -20,6 +20,24 @@
 
 
 def per_device(lender_block, confidence, lender_factors):
+
+    def _play_zones(u_in):
+        formed = jax.lax.psum(1, "shard")
+        placed = jax.lax.axis_index("shard")
+        taken_in, ready = (formed, placed)
+        vec_out = u_in.shape[0] // taken_in
+        state_next = list(u_in.shape)
+        state_next[0] = vec_out
+        earlier = state_next[0]
+        state_next[0] = earlier * taken_in
+        seen_now = jnp.zeros(state_next, u_in.dtype)
+        for w in [*range(taken_in)]:
+            new = lax.dynamic_slice_in_dim(u_in, (ready ^ w) * vec_out, vec_out, axis=0)
+            if w:
+                new = jax.lax.ppermute(new, "shard", [(at, at ^ w) for at in range(taken_in)])
+            seen_now = lax.dynamic_update_slice_in_dim(seen_now, new, (ready ^ w) * earlier, axis=0)
+        return seen_now
+
     shards = lax.axis_size("shard")
     blocks, lists = lender_block.shape
     tile = confidence.shape[2]
@@ -41,7 +59,7 @@
         jnp.zeros((shards * slots,), jnp.int32).at[slot_index].set(within).reshape(shards, slots)
     )
     table = lender_factors.reshape(owned, tile, rank)
-    incoming = lax.all_to_all(requests, "shard", split_axis=0, concat_axis=0, tiled=True)
+    incoming = _play_zones(requests)
     replies = lax.all_to_all(table[incoming], "shard", split_axis=0, concat_axis=0, tiled=True)
     fetched = replies.reshape(shards * slots, tile, rank)[slot_index].reshape(
         blocks, lists, tile, rank

time: 417 us -> 423 us (1.014)
  starting transfers between devices: 9.46 us -> 25.3 us
  blocking collectives: 13.6 us -> 0 us
  waiting for transfers between devices: 297 us -> 305 us
  local copies, waits for them, and re-layouts: 35.2 us -> 30.1 us
    ppermute x0 -> x7, starting transfers between devices: none -> 14.4 us  [_play_zones(): jax.lax.ppermute(new, 'shard', [(at, at ^ w) for at in range(taken_in)])]
    all_to_all x1 -> x0, blocking collectives: 13.6 us -> none  [per_device(): lax.all_to_all(requests, 'shard', split_axis=0, concat_axis=0, tiled=True)]
    ppermute x0 -> x7, waiting for transfers between devices: none -> 6.25 us  [_play_zones(): jax.lax.ppermute(new, 'shard', [(at, at ^ w) for at in range(taken_in)])]
    unnamed x7 -> x6, local copies, waits for them, and re-layouts: 4.71 us -> 0.02 us
  transfers between devices with their start and end apart: 4 -> 11, of which waited for: 4 -> 7; matrix products, arithmetic and copies ran while one was open for 5% -> 3% of each run, Pallas kernels for 0% -> 0%
where the time goes in v1:
time: 423 us; the launch traced here: 422 us
  waiting for transfers between devices  305 us (72%)
  matrix products  40.4 us (10%)
  local copies, waits for them, and re-layouts  30.1 us (7%)
  starting transfers between devices  25.3 us (6%)
  between operations  14.2 us (3%)
  other arithmetic  6.93 us (2%)
    all_to_all x1, waiting for transfers between devices, per_device(): lax.all_to_all(outgoing.reshape(shards, slots, tile, rank), 'shard', spli...  136 us
    psum x1, waiting for transfers between devices, per_device(): total = lax.psum(owner_sum, 'rep')  83.7 us
    all_to_all x1, waiting for transfers between devices, per_device(): lax.all_to_all(table[incoming], 'shard', split_axis=0, concat_axis=0, til...  66.5 us
    dot_general x3, matrix products, apply_system(): jnp.einsum('bktl,bklr->btr', weighted, fetched, preferred_element_type=jn...  16 us
    ppermute x7, starting transfers between devices, _play_zones(): jax.lax.ppermute(new, 'shard', [(at, at ^ w) for at in range(taken_in)])  14.4 us
    psum x1, waiting for transfers between devices, per_device(): gram = lax.psum(local_gram, 'shard')  12.1 us
    dot_general x1, matrix products, per_device(): jnp.dot(selector, returned.reshape(shards * slots, tile * rank), precisio...  10.8 us
  transfers between devices with their start and end apart: 11, of which 7 were waited for; matrix products, arithmetic and copies ran while one was open for 3% of the time, Pallas kernels for 0%

profile of v1, /device:TPU:0, one launch (start us, length us, event | category | flops | bytes accessed | tf_op | source)
XLA Modules:
  0.0 421.8 jit_solution(17701941789632341092)
XLA Ops:
  7.2 0.9 reshape.194
  8.1 0.8 reshape.193
  8.9 0.1 fusion.50
  9.0 0.2 select_reduce_fusion
  9.2 0.6 scatter_custom_fusion
  9.9 0.1 reshape.195
  10.0 6.1 %collective-permute-start.6 = (s32[1,6]{1,0:T(1,128)S(1)}, s32[1,6]{1,0:T(1,128)S(1)}, u32[]{:S(2)}, u32[]{:S(2)}) collective-permute-start(s32[1,6]{1,0:T(1,128)S(1)} %get-tuple-element.8), channel_id=1, source_target_pairs={{0,28},{4,24},{8,20},{12,16},{16,12},{20,8},{24,4},{28,0},{1,29},{... | collective-permute-start | bytes 80 | tf_op jit(solution)/shard_map/ppermute | solution.py:37
  16.0 0.2 collective-permute-start.5
  16.3 0.8 collective-permute-start.4
  17.0 2.0 collective-permute-start.3
  19.1 1.6 collective-permute-start
  20.7 1.9 collective-permute-done
  22.6 1.4 collective-permute-start.1
  24.0 2.2 collective-permute-done.1
  26.2 2.3 collective-permute-start.2
  28.5 2.2 collective-permute-done.2
  30.9 0.1 reshape.204
  31.0 2.7 gather_fusion
  33.7 5.9 %all-to-all-start = ((bf16[8,6,256,128]{3,2,1,0:T(8,128)(2,1)}), bf16[8,6,256,128]{3,2,1,0:T(8,128)(2,1)}, u32[]{:S(2)}, u32[]{:S(2)}) async-start(bf16[8,6,256,128]{3,2,1,0:T(8,128)(2,1)} %bitcast.101), calls=%async_computation | async-start | bytes 6291456 | tf_op jit(solution)/shard_map/all_to_all | solution.py:63
  39.7 1.4 fusion.55
  41.1 66.5 %all-to-all-done = bf16[8,6,256,128]{3,2,1,0:T(8,128)(2,1)} async-done(((bf16[8,6,256,128]{3,2,1,0:T(8,128)(2,1)}), bf16[8,6,256,128]{3,2,1,0:T(8,128)(2,1)}, u32[]{:S(2)}, u32[]{:S(2)}) %all-to-all-start) | async-done | bytes 3145760 | tf_op jit(solution)/shard_map/all_to_all | solution.py:63
  107.6 3.8 gather_fusion.1
  111.4 3.5 convolution_bitcast_fusion
  115.0 4.8 %fusion.18 = f32[3,256,128]{1,2,0:T(8,128)S(1)} fusion(bf16[3,8,256,128]{3,2,1,0:T(8,128)(2,1)} %bitcast.103, bf16[3,8,256,256]{3,2,1,0:T(8,128)(2,1)} %param.4, f32[3,256,128]{1,2,0:T(8,128)S(1)} %convolution_bitcast_fusion), kind=kOutput, calls=%fused_computation.20 | convolution fusion | flops 810123264 | bytes 5505024 | tf_op jit(solution)/shard_map/bktl,bklr->btr/dot_general | solution.py:14
  119.7 12.1 %all-reduce.3.cloned.1.call-done = f32[128,128]{1,0:T(8,128)} async-done(((f32[128,128]{1,0:T(8,128)}), f32[128,128]{1,0:T(8,128)}) %all-reduce.3.cloned.1.call-update) | async-done | bytes 65552 | tf_op jit(solution)/shard_map/psum | solution.py:51
  131.8 1.4 multiply_reduce_fusion.3
  133.3 0.1 multiply_reduce_fusion.2
  133.4 0.1 multiply_add_fusion.2
  133.4 5.5 %fusion.21 = f32[3,256,128]{1,2,0:T(8,128)} fusion(bf16[3,8,256,128]{3,2,1,0:T(8,128)(2,1)} %bitcast.104, bf16[3,8,256,256]{3,2,1,0:T(8,128)(2,1)} %param.4, f32[3,256,128]{1,2,0:T(8,128)S(1)} %multiply_add_fusion.2), kind=kOutput, calls=%fused_computation.21 | convolution fusion | flops 810123264 | bytes 5505024 | tf_op jit(solution)/shard_map/bktl,bklr->btr/dot_general | solution.py:14
  139.0 1.6 multiply_reduce_fusion.1
  140.5 0.1 multiply_reduce_fusion
  140.6 0.8 multiply_add_fusion.1
  141.5 5.7 %fusion.24 = f32[3,256,128]{1,2,0:T(8,128)} fusion(bf16[3,8,256,128]{3,2,1,0:T(8,128)(2,1)} %bitcast.105, bf16[3,8,256,256]{3,2,1,0:T(8,128)(2,1)} %param.4, f32[3,256,128]{1,2,0:T(8,128)} %multiply_add_fusion.1), kind=kOutput, calls=%fused_computation.22 | convolution fusion | flops 810123264 | bytes 5505024 | tf_op jit(solution)/shard_map/bktl,bklr->btr/dot_general | solution.py:14
  147.1 1.6 fusion.31
  148.7 1.1 multiply_add_fusion
  149.8 4.1 fusion.32
  153.9 3.6 copy.26
  157.5 3.4 broadcast_in_dim.8
  160.9 7.9 %scatter_fusion = f32[48,256,128]{2,1,0:T(8,128)} fusion(f32[48,256,128]{2,1,0:T(8,128)} %broadcast_in_dim.8, s32[24]{0:T(128)S(1)} %fusion.52, f32[24,256,128]{2,1,0:T(8,128)} %copy.26), kind=kCustom, calls=%fused_computation.3 | custom fusion | bytes 9437280 | tf_op jit(solution)/shard_map/scatter | solution.py:87
  168.9 4.8 %all-to-all-start.1 = ((f32[8,6,256,128]{3,2,1,0:T(8,128)}), f32[8,6,256,128]{3,2,1,0:T(8,128)}, u32[]{:S(2)}, u32[]{:S(2)}) async-start(f32[8,6,256,128]{3,2,1,0:T(8,128)} %bitcast.99), calls=%async_computation.1 | async-start | bytes 12582912 | tf_op jit(solution)/shard_map/all_to_all | solution.py:89
  173.6 0.2 all-reduce.5.cloned.1.call-start
  173.9 0.1 eq.31
  173.9 136.2 %all-to-all-done.1 = f32[8,6,256,128]{3,2,1,0:T(8,128)} async-done(((f32[8,6,256,128]{3,2,1,0:T(8,128)}), f32[8,6,256,128]{3,2,1,0:T(8,128)}, u32[]{:S(2)}, u32[]{:S(2)}) %all-to-all-start.1) | async-done | bytes 6291488 | tf_op jit(solution)/shard_map/all_to_all | solution.py:89
  310.2 10.8 %fusion.3 = f32[32,32768]{1,0:T(8,128)} fusion(f32[6,8,256,128]{3,2,1,0:T(8,128)} %bitcast.37, s32[48]{0:T(128)S(1)} %eq.31), kind=kOutput, calls=%fused_computation.10 | convolution fusion | flops 603981312 | bytes 10485952 | tf_op jit(solution)/shard_map/dot_general | solution.py:99
  321.0 0.9 copy.25
  322.0 83.7 %all-reduce.5.cloned.1.call-done = f32[32,32768]{1,0:T(8,128)} async-done(((f32[32,32768]{1,0:T(8,128)}), f32[32,32768]{1,0:T(8,128)}) %all-reduce.5.cloned.1.call-update) | async-done | bytes 4194320 | tf_op jit(solution)/shard_map/psum | solution.py:105
  405.6 4.4 %broadcast_multiply_fusion = f32[32,32768]{1,0:T(8,128)} fusion(f32[32,32768]{1,0:T(8,128)} %all-reduce.5.cloned.1.call-done), kind=kLoop, calls=%fused_computation.19 | loop fusion | flops 1048576 | bytes 8388608 | tf_op jit(solution)/shard_map/div | solution.py:107
  410.1 4.9 %div.83 = f32[8192,128]{1,0:T(8,128)} reshape(f32[32,32768]{1,0:T(8,128)} %broadcast_multiply_fusion) | data formatting | bytes 8388608 | tf_op jit(solution)/shard_map/div | solution.py:107
  (34 shorter events, 0.5 us)
Async XLA Ops:
  7.2 23.8 %copy-start = (bf16[8192,128]{1,0:T(8,128)(2,1)S(1)}, bf16[8192,128]{1,0:T(8,128)(2,1)}, u32[]{:S(2)}) copy-start(bf16[8192,128]{1,0:T(8,128)(2,1)} %param.5) | copy-start | bytes 6291460
  10.0 20.8 %collective-permute-start.6 = (s32[1,6]{1,0:T(1,128)S(1)}, s32[1,6]{1,0:T(1,128)S(1)}, u32[]{:S(2)}, u32[]{:S(2)}) collective-permute-start(s32[1,6]{1,0:T(1,128)S(1)} %get-tuple-element.8), channel_id=1, source_target_pairs={{0,28},{4,24},{8,20},{12,16},{16,12},{20,8},{24,4},{28,0},{1,29},{... | collective-permute-start | bytes 80 | tf_op jit(solution)/shard_map/ppermute | solution.py:37
  16.0 14.7 %collective-permute-start.5 = (s32[1,6]{1,0:T(1,128)S(1)}, s32[1,6]{1,0:T(1,128)S(1)}, u32[]{:S(2)}, u32[]{:S(2)}) collective-permute-start(s32[1,6]{1,0:T(1,128)S(1)} %get-tuple-element.9), channel_id=1, source_target_pairs={{0,24},{4,28},{8,16},{12,20},{16,8},{20,12},{24,0},{28,4},{1,25},{... | collective-permute-start | bytes 80 | tf_op jit(solution)/shard_map/ppermute | solution.py:37
  16.3 14.5 %collective-permute-start.4 = (s32[1,6]{1,0:T(1,128)S(1)}, s32[1,6]{1,0:T(1,128)S(1)}, u32[]{:S(2)}, u32[]{:S(2)}) collective-permute-start(s32[1,6]{1,0:T(1,128)S(1)} %get-tuple-element.10), channel_id=1, source_target_pairs={{0,20},{4,16},{8,28},{12,24},{16,4},{20,0},{24,12},{28,8},{1,21},{... | collective-permute-start | bytes 80 | tf_op jit(solution)/shard_map/ppermute | solution.py:37
  17.0 13.7 %collective-permute-start.3 = (s32[1,6]{1,0:T(1,128)S(1)}, s32[1,6]{1,0:T(1,128)S(1)}, u32[]{:S(2)}, u32[]{:S(2)}) collective-permute-start(s32[1,6]{1,0:T(1,128)S(1)} %get-tuple-element.11), channel_id=1, source_target_pairs={{0,16},{4,20},{8,24},{12,28},{16,0},{20,4},{24,8},{28,12},{1,17},{... | collective-permute-start | bytes 80 | tf_op jit(solution)/shard_map/ppermute | solution.py:37
  19.1 3.6 collective-permute-start
  22.6 3.6 collective-permute-start.1
  26.2 4.5 %collective-permute-start.2 = (s32[1,6]{1,0:T(1,128)S(1)}, s32[1,6]{1,0:T(1,128)S(1)}, u32[]{:S(2)}, u32[]{:S(2)}) collective-permute-start(s32[1,6]{1,0:T(1,128)S(1)} %get-tuple-element.12), channel_id=1, source_target_pairs={{0,12},{4,8},{8,4},{12,0},{16,28},{20,24},{24,20},{28,16},{1,13},{... | collective-permute-start | bytes 80 | tf_op jit(solution)/shard_map/ppermute | solution.py:37
  33.7 73.9 %all-to-all-start = ((bf16[8,6,256,128]{3,2,1,0:T(8,128)(2,1)}), bf16[8,6,256,128]{3,2,1,0:T(8,128)(2,1)}, u32[]{:S(2)}, u32[]{:S(2)}) async-start(bf16[8,6,256,128]{3,2,1,0:T(8,128)(2,1)} %bitcast.101), calls=%async_computation | async-start | bytes 6291456 | tf_op jit(solution)/shard_map/all_to_all | solution.py:63
  39.6 92.2 %all-reduce.3.cloned.1.call-start = ((), (), s32[]{:S(2)}) async-start(), calls=%async_computation.2 | async-start | bytes 131072 | tf_op jit(solution)/shard_map/psum | solution.py:51
  133.4 5.5 %copy-start.2 = (f32[128,128]{1,0:T(8,128)S(1)}, f32[128,128]{1,0:T(8,128)}, u32[]{:S(2)}) copy-start(f32[128,128]{1,0:T(8,128)} %all-reduce.3.cloned.1.call-done) | copy-start | bytes 196612
  141.5 5.7 %copy-start.1 = (f32[3,256,128]{1,2,0:T(8,128)S(1)}, f32[3,256,128]{1,2,0:T(8,128)}, u32[]{:S(2)}) copy-start(f32[3,256,128]{1,2,0:T(8,128)} %multiply_add_fusion.1) | copy-start | bytes 1179652
  168.9 141.3 %all-to-all-start.1 = ((f32[8,6,256,128]{3,2,1,0:T(8,128)}), f32[8,6,256,128]{3,2,1,0:T(8,128)}, u32[]{:S(2)}, u32[]{:S(2)}) async-start(f32[8,6,256,128]{3,2,1,0:T(8,128)} %bitcast.99), calls=%async_computation.1 | async-start | bytes 12582912 | tf_op jit(solution)/shard_map/all_to_all | solution.py:89
  173.6 232.0 %all-reduce.5.cloned.1.call-start = ((), (), s32[]{:S(2)}) async-start(), calls=%async_computation.3 | async-start | bytes 8388608 | tf_op jit(solution)/shard_map/psum | solution.py:105
Sparse Core Ops, SparseCore 0:
  44.4 87.3 all-reduce.2
  321.2 84.4 all-reduce.4
